TPU v7x, 32 devices: a whole 2x2x4 slice. The times are simulated.
32 devices in a mesh: cluster: 4 (over x, core), leaf: 8 (over z, y).
Axes of the slice: x: 2, y: 2, z: 4, core: 2. Of those that a mesh axis runs over, the one named last changes fastest.
Arguments:
- probes: float32 [32768, 512], P(('cluster', 'leaf')), may hold values from -6 to 6
- dense_leaf: float32 [32768, 1024], P(('cluster', 'leaf')), may hold values from -0.1875 to 0.1875
- leaf_basis: float32 [32768, 128], P(('cluster', 'leaf')), may hold values from -0.1875 to 0.1875
- sibling_cores: float32 [32, 8, 128, 128], P(('cluster', 'leaf')), may hold values from -0.5 to 0.5
- transfer: float32 [32, 128, 128], P(('cluster', 'leaf')), may hold values from -0.5 to 0.5
- cluster_cores: float32 [4, 4, 128, 128], P('cluster'), may hold values from -0.1875 to 0.1875
Outputs:
- product: float32 [32768, 512], P(('cluster', 'leaf'))
All inputs are finite; a program needn't handle non-finite values.
Results may differ from a plain program's by a relative error of at most 0.00005.
Values sent between devices are 32-bit elements; how exact they have to be, the bound alone decides.
No kernel may reach another device: no remote copies, remote signals or barrier semaphores. Data moves between devices by JAX's collectives and lax.ppermute only.
A program may use at most 128 MiB of HBM per device.

v0:
```python
import jax
import jax.numpy as jnp
from jax import lax
from jax.sharding import PartitionSpec as P

HI = lax.Precision.HIGHEST


def local(probes, dense_leaf, leaf_basis, sibling_cores, transfer, cluster_cores):
    own = lax.axis_index("leaf")
    cown = lax.axis_index("cluster")
    cores = sibling_cores[0]
    trans = transfer[0]
    outer_cores = cluster_cores[0]
    rank_two = trans.shape[1]
    near = jnp.dot(dense_leaf, probes, precision=HI) + jnp.dot(dense_leaf.T, probes, precision=HI)
    coef = jnp.dot(leaf_basis.T, probes, precision=HI)
    turned = lax.all_to_all(cores, "leaf", split_axis=0, concat_axis=0, tiled=True)
    used = cores + jnp.transpose(turned, (0, 2, 1))
    piece = lax.all_gather(coef[None], "leaf", axis=0, tiled=True)
    count = piece.shape[0]
    block = used
    keep = (jnp.arange(count, dtype=jnp.int32) != own).astype(jnp.float32)
    block = block * keep[:, None, None]
    sib = jnp.einsum("jab,jbp->ap", block, piece, precision=HI)
    local_g = jnp.dot(trans.T, coef, precision=HI)
    nclu = outer_cores.shape[0]
    bkeep = (jnp.arange(nclu, dtype=jnp.int32) != cown).astype(jnp.float32)[:, None, None]
    masked = outer_cores * bkeep
    g_whole = lax.psum(local_g, "leaf")
    gathered = lax.all_gather(g_whole[None], "cluster", axis=0, tiled=True)
    front = jnp.einsum("dab,dbp->ap", masked, gathered, precision=HI)
    number = rank_two * lax.axis_size("cluster") // rank_two
    block = masked
    terms = jnp.einsum("dba,bp->dap", block, g_whole, precision=HI)
    field = front + lax.psum_scatter(
        terms.reshape(number * rank_two, g_whole.shape[1]),
        "cluster",
        scatter_dimension=0,
        tiled=True,
    )
    total = sib + jnp.dot(trans, field, precision=HI)
    return near + jnp.dot(leaf_basis, total, precision=HI)


def solution(mesh):
    return jax.shard_map(
        local,
        mesh=mesh,
        in_specs=(
            P(("cluster", "leaf"), None),
            P(("cluster", "leaf"), None),
            P(("cluster", "leaf"), None),
            P(("cluster", "leaf"), None, None, None),
            P(("cluster", "leaf"), None, None),
            P("cluster", None, None, None),
        ),
        out_specs=P(("cluster", "leaf"), None),
        check_vma=False,
    )
```

profile of v0, /device:TPU:0, one launch (start us, length us, event | category | flops | bytes accessed | tf_op | source)
XLA Modules:
  0.0 197.5 jit_solution(9313554170039844846)
XLA Ops:
  6.5 1.6 copy-done
  8.1 2.4 %fusion.10 = f32[128,512]{1,0:T(8,128)S(1)} fusion(f32[1024,128]{1,0:T(8,128)} %param.8, f32[1024,512]{1,0:T(8,128)S(1)} %copy-done), kind=kOutput, calls=%fused_computation.18 | convolution fusion | flops 805306368 | bytes 2883584 | tf_op jit(solution)/shard_map/dot_general | solution.py:17
  10.6 1.3 convolution_bitcast_fusion.3
  11.9 0.0 all-reduce.2.cloned.1.call-update
  11.9 0.0 all-gather.7.cloned.1.call-start
  11.9 73.8 %all-reduce.2.cloned.1.call-done = f32[128,512]{0,1:T(8,128)} async-done(((f32[128,512]{0,1:T(8,128)}), f32[128,512]{0,1:T(8,128)}) %all-reduce.2.cloned.1.call-update) | async-done | bytes 262160 | tf_op jit(solution)/shard_map/psum | solution.py:30
  85.8 0.0 reduce-scatter.2.cloned.1.call-start
  85.8 0.1 copy.10
  86.0 0.1 bitcast_multiply_fusion
  86.1 2.9 %fusion.11 = f32[512,512]{1,0:T(8,128)} fusion(f32[512,128]{1,0:T(8,128)S(1)} %bitcast.52, f32[128,512]{0,1:T(8,128)} %all-reduce.2.cloned.1.call-done), kind=kOutput, calls=%fused_computation.19 | convolution fusion | flops 402653184 | bytes 1572864 | tf_op jit(solution)/shard_map/dba,bp->dap/dot_general | solution.py:35
  89.0 0.0 reduce-scatter.2.cloned.1.call-update
  89.1 0.0 all-gather.5.cloned.1.call-start
  89.1 0.5 all-gather.5.cloned.1.call-update
  89.6 1.0 copy.9
  90.6 4.3 %all-to-all-start = ((f32[8,128,128]{1,2,0:T(8,128)}), f32[8,128,128]{1,2,0:T(8,128)}, u32[]{:S(2)}, u32[]{:S(2)}) async-start(f32[8,128,128]{1,2,0:T(8,128)} %copy.9), calls=%async_computation | async-start | bytes 1048576 | tf_op jit(solution)/shard_map/all_to_all | solution.py:18
  95.0 9.6 %fusion.8 = f32[1024,512]{1,0:T(8,128)} fusion(f32[1024,1024]{1,0:T(8,128)} %param.7, f32[1024,512]{1,0:T(8,128)S(1)} %copy-done), kind=kOutput, calls=%fused_computation.16 | convolution fusion | flops 6442450944 | bytes 8388608 | tf_op jit(solution)/shard_map/dot_general | solution.py:16
  104.6 9.6 %fusion.9 = f32[1024,512]{1,0:T(8,128)} fusion(f32[1024,1024]{1,0:T(8,128)} %param.7, f32[1024,512]{1,0:T(8,128)S(1)} %copy-done), kind=kOutput, calls=%fused_computation.17 | convolution fusion | flops 6442450944 | bytes 8388608 | tf_op jit(solution)/shard_map/dot_general | solution.py:16
  114.2 1.6 copy.14
  115.8 15.0 %reduce-scatter.2.cloned.1.call-done = f32[128,512]{1,0:T(8,128)} async-done(((f32[512,512]{1,0:T(8,128)}), f32[128,512]{1,0:T(8,128)}) %reduce-scatter.2.cloned.1.call-update) | async-done | bytes 262160 | tf_op jit(solution)/shard_map/reduce_scatter | solution.py:36
  130.7 2.4 %fusion.1 = f32[128,512]{1,0:T(8,128)} fusion(f32[128,512]{1,0:T(8,128)} %reduce-scatter.2.cloned.1.call-done, f32[4,128,128]{1,2,0:T(8,128)S(1)} %bitcast_multiply_fusion, f32[4,128,512]{2,1,0:T(8,128)S(1)} %bitcast.51), kind=kOutput, calls=%fused_computation.6 | convolution fusion | flops 402718720 | bytes 1835008 | tf_op jit(solution)/shard_map/dab,dbp->ap/dot_general | solution.py:32
  133.1 48.7 %all-gather.5.cloned.1.call-done = f32[1024,512]{1,0:T(8,128)} async-done(((f32[128,512]{1,0:T(8,128)}), f32[1024,512]{1,0:T(8,128)}) %all-gather.5.cloned.1.call-update) | async-done | bytes 2097168 | tf_op jit(solution)/shard_map/all_gather | solution.py:20
  181.8 3.4 %convolution_bitcast_fusion = f32[128,512]{1,0:T(8,128)S(1)} fusion(f32[8,128,512]{2,1,0:T(8,128)} %bitcast.53, f32[8,128,128]{1,2,0:T(8,128)} %all-to-all-done, f32[8]{0:T(128)S(1)} %compare_convert_fusion.1, f32[1,8,128,128]{3,2,1,0:T(8,128)} %param.9), kind=kOutput, calls=%fused_computation.1 | convolution fusion | flops 805568512 | bytes 3407904 | tf_op jit(solution)/shard_map/jab,jbp->ap/dot_general | solution.py:25
  185.2 1.3 fusion
  186.6 4.4 %bitcast_add_fusion = f32[1024,512]{1,0:T(8,128)} fusion(f32[1024,512]{1,0:T(8,128)S(1)} %copy-done.2, f32[1024,512]{1,0:T(8,128)S(1)} %copy-done.1, f32[128,512]{1,0:T(8,128)S(1)} %fusion, f32[1024,128]{1,0:T(8,128)} %param.8), kind=kOutput, calls=%fused_computation | convolution fusion | flops 806354944 | bytes 7077888 | tf_op jit(solution)/shard_map/dot_general | solution.py:43
  (19 shorter events, 0.1 us)
Async XLA Ops:
  6.5 1.6 copy-start
  6.5 4.0 %copy-start.6 = (f32[1,128,128]{2,1,0:T(8,128)S(1)}, f32[1,128,128]{2,1,0:T(8,128)}, u32[]{:S(2)}) copy-start(f32[1,128,128]{2,1,0:T(8,128)} %param.10) | copy-start | bytes 196612
  6.5 79.3 %copy-start.5 = (f32[1,4,128,128]{3,2,1,0:T(8,128)S(1)}, f32[1,4,128,128]{3,2,1,0:T(8,128)}, u32[]{:S(2)}) copy-start(f32[1,4,128,128]{3,2,1,0:T(8,128)} %param.11) | copy-start | bytes 786436
  6.5 79.2 %all-reduce.2.cloned.1.call-start = ((), (), s32[]{:S(2)}) async-start(), calls=%async_computation.2 | async-start | bytes 524288 | tf_op jit(solution)/shard_map/psum | solution.py:30
  10.5 78.5 %copy-start.3 = (f32[128,512]{1,0:T(8,128)}, f32[128,512]{1,0:T(8,128)S(1)}, u32[]{:S(2)}) copy-start(f32[128,512]{1,0:T(8,128)S(1)} %fusion.10) | copy-start | bytes 786436
  11.9 102.3 %all-gather.7.cloned.1.call-start = ((), (), s32[]{:S(2)}) async-start(), calls=%async_computation.5 | async-start | bytes 1310720 | tf_op jit(solution)/shard_map/all_gather | solution.py:31
  85.8 3.9 %copy-start.4 = (f32[1,8,128,128]{3,2,1,0:T(8,128)S(1)}, f32[1,8,128,128]{3,2,1,0:T(8,128)}, u32[]{:S(2)}) copy-start(f32[1,8,128,128]{3,2,1,0:T(8,128)} %param.9) | copy-start | bytes 1572868
  85.8 44.9 %reduce-scatter.2.cloned.1.call-start = ((), (), s32[]{:S(2)}) async-start(), calls=%async_computation.3 | async-start | bytes 1310720 | tf_op jit(solution)/shard_map/reduce_scatter | solution.py:36
  89.1 92.8 %all-gather.5.cloned.1.call-start = ((), (), s32[]{:S(2)}) async-start(), calls=%async_computation.4 | async-start | bytes 2359296 | tf_op jit(solution)/shard_map/all_gather | solution.py:20
  90.6 42.5 %all-to-all-start = ((f32[8,128,128]{1,2,0:T(8,128)}), f32[8,128,128]{1,2,0:T(8,128)}, u32[]{:S(2)}, u32[]{:S(2)}) async-start(f32[8,128,128]{1,2,0:T(8,128)} %copy.9), calls=%async_computation | async-start | bytes 1048576 | tf_op jit(solution)/shard_map/all_to_all | solution.py:18
  181.8 4.7 %copy-start.1 = (f32[1024,512]{1,0:T(8,128)S(1)}, f32[1024,512]{1,0:T(8,128)}, u32[]{:S(2)}) copy-start(f32[1024,512]{1,0:T(8,128)} %fusion.9) | copy-start | bytes 6291460
  181.8 4.7 %copy-start.2 = (f32[1024,512]{1,0:T(8,128)S(1)}, f32[1024,512]{1,0:T(8,128)}, u32[]{:S(2)}) copy-start(f32[1024,512]{1,0:T(8,128)} %fusion.8) | copy-start | bytes 6291460
Sparse Core Ops, SparseCore 0:
  12.0 73.7 all-reduce.1
  87.3 16.0 all-gather.6
  105.9 24.7 reduce-scatter.1
  132.7 49.0 all-gather.4
where the time goes:
time: 198 us; the launch traced here: 197 us
  waiting for transfers between devices  138 us (70%)
  matrix products  37.3 us (19%)
  between operations  13.3 us (7%)
  starting transfers between devices  4.44 us (2%)
  local copies, waits for them, and re-layouts  4.31 us (2%)
    psum x1, waiting for transfers between devices, local(): g_whole = lax.psum(local_g, 'leaf')  73.8 us
    all_gather x1, waiting for transfers between devices, local(): piece = lax.all_gather(coef[None], 'leaf', axis=0, tiled=True)  48.7 us
    reduce_scatter x1, waiting for transfers between devices, local(): lax.psum_scatter(terms.reshape(number * rank_two, g_whole.shape[1]), 'clu...  15 us
    dot_general x1, matrix products, local(): jnp.dot(dense_leaf.T, probes, precision=HI)  9.6 us
    dot_general x1, matrix products, local(): jnp.dot(dense_leaf, probes, precision=HI)  9.59 us
    dot_general x1, matrix products, local(): return near + jnp.dot(leaf_basis, total, precision=HI)  4.38 us
    all_to_all x1, starting transfers between devices, local(): lax.all_to_all(cores, 'leaf', split_axis=0, concat_axis=0, tiled=True)  4.32 us
  transfers between devices with their start and end apart: 5, of which 3 were waited for; matrix products, arithmetic and copies ran while one was open for 14% of the time, Pallas kernels for 0%

commit v1 on v0

--- a/solution.py
+++ b/solution.py
@@ -2,8 +2,21 @@
 import jax.numpy as jnp
 from jax import lax
 from jax.sharding import PartitionSpec as P
+from jax.lax import axis_index, ppermute, psum
 
 HI = lax.Precision.HIGHEST
+
+
+def expand_routes_all(sheet):
+    fan = psum(1, axis_name="leaf")
+    column = tuple(((j0, (j0 + 1) % fan) for j0 in range(fan)))
+    part_now = [None] * fan
+    part_now[fan - 1] = sheet
+    for jj in range(fan - 2, -1, -1):
+        part_now[jj] = ppermute(part_now[jj + 1], "leaf", column)
+    piece_out = jnp.concatenate(part_now, axis=0)
+    local_next = axis_index("leaf")
+    return jnp.roll(piece_out, shift=(local_next + 1) * sheet.shape[0], axis=0)
 
 
 def local(probes, dense_leaf, leaf_basis, sibling_cores, transfer, cluster_cores):
@@ -17,7 +30,7 @@
     coef = jnp.dot(leaf_basis.T, probes, precision=HI)
     turned = lax.all_to_all(cores, "leaf", split_axis=0, concat_axis=0, tiled=True)
     used = cores + jnp.transpose(turned, (0, 2, 1))
-    piece = lax.all_gather(coef[None], "leaf", axis=0, tiled=True)
+    piece = expand_routes_all(coef[None])
     count = piece.shape[0]
     block = used
     keep = (jnp.arange(count, dtype=jnp.int32) != own).astype(jnp.float32)

time: 198 us -> 177 us (0.89)
  waiting for transfers between devices: 138 us -> 89.8 us
  local copies, waits for them, and re-layouts: 4.31 us -> 24.5 us
  starting transfers between devices: 4.44 us -> 12.9 us
    all_gather x1 -> x0, waiting for transfers between devices: 48.7 us -> none  [local(): piece = lax.all_gather(coef[None], 'leaf', axis=0, tiled=True)]
    ppermute x0 -> x7, waiting for transfers between devices: none -> 30.4 us  [expand_routes_all(): part_now[jj] = ppermute(part_now[jj + 1], 'leaf', column)]
    unnamed x15 -> x34, local copies, waits for them, and re-layouts: 1.73 us -> 20.1 us
    psum x1, waiting for transfers between devices: 73.8 us -> 59.1 us  [local(): g_whole = lax.psum(local_g, 'leaf')]
    reduce_scatter x1, waiting for transfers between devices: 15 us -> 0.2 us  [local(): lax.psum_scatter(terms.reshape(number * rank_two, g_whole.shape[1]), 'clu...]
    ppermute x0 -> x7, starting transfers between devices: none -> 6.78 us  [expand_routes_all(): part_now[jj] = ppermute(part_now[jj + 1], 'leaf', column)]
  transfers between devices with their start and end apart: 5 -> 11, of which waited for: 3 -> 6; matrix products, arithmetic and copies ran while one was open for 14% -> 27% of each run, Pallas kernels for 0% -> 0%
where the time goes in v1:
time: 177 us
  waiting for transfers between devices  89.8 us (51%)
  matrix products  36.1 us (20%)
  local copies, waits for them, and re-layouts  24.5 us (14%)
  between operations  13.3 us (8%)
  starting transfers between devices  12.9 us (7%)
    psum x1, waiting for transfers between devices, local(): g_whole = lax.psum(local_g, 'leaf')  59.1 us
    ppermute x7, waiting for transfers between devices, expand_routes_all(): part_now[jj] = ppermute(part_now[jj + 1], 'leaf', column)  30.4 us
    unnamed x34, local copies, waits for them, and re-layouts  20.1 us
    dot_general x1, matrix products, local(): jnp.dot(dense_leaf, probes, precision=HI)  9.94 us
    dot_general x1, matrix products, local(): jnp.dot(dense_leaf.T, probes, precision=HI)  8.14 us
    ppermute x7, starting transfers between devices, expand_routes_all(): part_now[jj] = ppermute(part_now[jj + 1], 'leaf', column)  6.78 us
    all_to_all x1, starting transfers between devices, local(): lax.all_to_all(cores, 'leaf', split_axis=0, concat_axis=0, tiled=True)  6 us
    dot_general x1, matrix products, local(): return near + jnp.dot(leaf_basis, total, precision=HI)  4.89 us
  transfers between devices with their start and end apart: 11, of which 6 were waited for; matrix products, arithmetic and copies ran while one was open for 27% of the time, Pallas kernels for 0%

profile of v1, /device:TPU:0, one launch (start us, length us, event | category | flops | bytes accessed | tf_op | source)
XLA Modules:
  0.0 176.6 jit_solution(17873722249513715591)
XLA Ops:
  6.5 1.6 copy-done
  8.1 2.4 %fusion.18 = f32[128,512]{1,0:T(8,128)S(1)} fusion(f32[1024,128]{1,0:T(8,128)} %param.8, f32[1024,512]{1,0:T(8,128)S(1)} %copy-done), kind=kOutput, calls=%fused_computation.37 | convolution fusion | flops 805306368 | bytes 2883584 | tf_op jit(solution)/shard_map/dot_general | solution.py:30
  10.5 3.0 %collective-permute-start = (f32[1,128,512]{2,1,0:T(8,128)S(1)}, f32[1,128,512]{2,1,0:T(8,128)S(1)}, u32[]{:S(2)}, u32[]{:S(2)}) collective-permute-start(f32[1,128,512]{2,1,0:T(8,128)S(1)} %bitcast.53), channel_id=1, source_target_pairs={{0,1},{1,2},{2,3},{3,4},{4,5},{5,6},{6,7},{7,0},{8,9},{9,10},{10,1... | collective-permute-start | bytes 786440 | tf_op jit(solution)/shard_map/ppermute | solution.py:16
  13.6 9.3 %collective-permute-done = f32[1,128,512]{2,1,0:T(8,128)S(1)} collective-permute-done((f32[1,128,512]{2,1,0:T(8,128)S(1)}, f32[1,128,512]{2,1,0:T(8,128)S(1)}, u32[]{:S(2)}, u32[]{:S(2)}) %collective-permute-start) | collective-permute-done | bytes 262176 | tf_op jit(solution)/shard_map/ppermute | solution.py:16
  22.9 2.2 %convolution_bitcast_fusion.2 = f32[128,512]{0,1:T(8,128)} fusion(f32[128,512]{1,0:T(8,128)S(1)} %fusion.18, f32[1,128,128]{2,1,0:T(8,128)} %param.10), kind=kOutput, calls=%fused_computation.6 | convolution fusion | flops 100663296 | bytes 589824 | tf_op jit(solution)/shard_map/dot_general | solution.py:39
  25.1 8.0 %collective-permute-done.1 = f32[1,128,512]{2,1,0:T(8,128)S(1)} collective-permute-done((f32[1,128,512]{2,1,0:T(8,128)S(1)}, f32[1,128,512]{2,1,0:T(8,128)S(1)}, u32[]{:S(2)}, u32[]{:S(2)}) %collective-permute-start.1) | collective-permute-done | bytes 262176 | tf_op jit(solution)/shard_map/ppermute | solution.py:16
  33.1 2.1 %copy.9 = f32[8,128,128]{1,2,0:T(8,128)} copy(f32[8,128,128]{2,1,0:T(8,128)} %bitcast.55) | data formatting | bytes 1048576 | tf_op jit(solution)/shard_map/squeeze | solution.py:25
  35.2 6.0 %all-to-all-start = ((f32[8,128,128]{1,2,0:T(8,128)}), f32[8,128,128]{1,2,0:T(8,128)}, u32[]{:S(2)}, u32[]{:S(2)}) async-start(f32[8,128,128]{1,2,0:T(8,128)} %copy.9), calls=%async_computation | async-start | bytes 1048576 | tf_op jit(solution)/shard_map/all_to_all | solution.py:31
  41.2 59.1 %all-reduce.2.cloned.1.call-done = f32[128,512]{0,1:T(8,128)} async-done(((f32[128,512]{0,1:T(8,128)}), f32[128,512]{0,1:T(8,128)}) %all-reduce.2.cloned.1.call-update) | async-done | bytes 262160 | tf_op jit(solution)/shard_map/psum | solution.py:43
  101.1 9.9 %fusion.16 = f32[1024,512]{1,0:T(8,128)} fusion(f32[1024,1024]{1,0:T(8,128)} %param.7, f32[1024,512]{1,0:T(8,128)S(1)} %copy-done), kind=kOutput, calls=%fused_computation.35 | convolution fusion | flops 6442450944 | bytes 8388608 | tf_op jit(solution)/shard_map/dot_general | solution.py:29
  112.6 8.1 %fusion.17 = f32[1024,512]{1,0:T(8,128)} fusion(f32[1024,1024]{1,0:T(8,128)S(1)} %copy-done.1, f32[1024,512]{1,0:T(8,128)S(1)} %copy-done), kind=kOutput, calls=%fused_computation.36 | convolution fusion | flops 6442450944 | bytes 8388608 | tf_op jit(solution)/shard_map/dot_general | solution.py:29
  123.4 6.8 %collective-permute-done.5 = f32[1,128,512]{2,1,0:T(8,128)} collective-permute-done((f32[1,128,512]{2,1,0:T(8,128)}, f32[1,128,512]{2,1,0:T(8,128)}, u32[]{:S(2)}, u32[]{:S(2)}) %collective-permute-start.5) | collective-permute-done | bytes 262176 | tf_op jit(solution)/shard_map/ppermute | solution.py:16
  130.2 3.0 %fusion.19 = f32[512,512]{1,0:T(8,128)} fusion(f32[512,128]{1,0:T(8,128)S(1)} %bitcast.54, f32[128,512]{0,1:T(8,128)} %all-reduce.2.cloned.1.call-done), kind=kOutput, calls=%fused_computation.38 | convolution fusion | flops 402653184 | bytes 1572864 | tf_op jit(solution)/shard_map/dba,bp->dap/dot_general | solution.py:48
  133.2 6.4 %collective-permute-done.6 = f32[1,128,512]{2,1,0:T(8,128)} collective-permute-done((f32[1,128,512]{2,1,0:T(8,128)}, f32[1,128,512]{2,1,0:T(8,128)}, u32[]{:S(2)}, u32[]{:S(2)}) %collective-permute-start.6) | collective-permute-done | bytes 262176 | tf_op jit(solution)/shard_map/ppermute | solution.py:16
  139.6 1.7 constant_dynamic-update-slice_fusion.15
  141.2 1.7 constant_dynamic-update-slice_fusion.14
  142.9 1.7 constant_dynamic-update-slice_fusion.13
  148.2 1.7 constant_dynamic-update-slice_fusion.7
  149.9 1.7 constant_dynamic-update-slice_fusion.6
  151.5 1.7 constant_dynamic-update-slice_fusion.5
  156.9 1.7 constant_dynamic-update-slice_fusion.1
  159.5 1.8 %fusion.8 = f32[128,512]{1,0:T(8,128)S(1)} fusion(f32[128,512]{1,0:T(8,128)} %reduce-scatter.2.cloned.1.call-done, f32[4,128,128]{1,2,0:T(8,128)} %copy-done.3, f32[4,128,512]{2,1,0:T(8,128)S(1)} %bitcast.52), kind=kOutput, calls=%fused_computation.8 | convolution fusion | flops 402718720 | bytes 1835008 | tf_op jit(solution)/shard_map/dab,dbp->ap/dot_general | solution.py:45
  161.7 3.4 %fusion.5 = f32[128,512]{1,0:T(8,128)S(1)} fusion(f32[128,512]{1,0:T(8,128)S(1)} %convolution_bitcast_fusion, f32[16,128,512]{2,1,0:T(8,128)} %constant_dynamic-update-slice_fusion, s32[]{:T(128)S(6)} %select_n.14, f32[8,128,128]{1,2,0:T(8,128)} %all-to-all-done, f32[8]{0:T(128)S(1)} %compare_convert_fusion.1, f32[1,8,128,128]{3,2,1,0:T(8,128)} %param.9), kind=kOutput, calls=%fused_computation.7 | convolution fusion | flops 805634048 | bytes 3670052 | tf_op jit(solution)/shard_map/jab,jbp->ap/dot_general | solution.py:38
  165.2 4.9 %bitcast_add_fusion = f32[1024,512]{1,0:T(8,128)} fusion(f32[1024,512]{1,0:T(8,128)} %fusion.16, f32[1024,512]{1,0:T(8,128)S(1)} %copy-done.2, f32[128,512]{1,0:T(8,128)S(1)} %fusion.5, f32[1024,128]{1,0:T(8,128)S(1)} %copy-done.4), kind=kOutput, calls=%fused_computation | convolution fusion | flops 806354944 | bytes 7077888 | tf_op jit(solution)/shard_map/dot_general | solution.py:56
  (50 shorter events, 13.6 us)
Async XLA Ops:
  6.5 1.6 copy-start
  6.5 93.7 %all-reduce.2.cloned.1.call-start = ((), (), s32[]{:S(2)}) async-start(), calls=%async_computation.2 | async-start | bytes 524288 | tf_op jit(solution)/shard_map/psum | solution.py:43
  10.5 12.4 %collective-permute-start = (f32[1,128,512]{2,1,0:T(8,128)S(1)}, f32[1,128,512]{2,1,0:T(8,128)S(1)}, u32[]{:S(2)}, u32[]{:S(2)}) collective-permute-start(f32[1,128,512]{2,1,0:T(8,128)S(1)} %bitcast.53), channel_id=1, source_target_pairs={{0,1},{1,2},{2,3},{3,4},{4,5},{5,6},{6,7},{7,0},{8,9},{9,10},{10,1... | collective-permute-start | bytes 786440 | tf_op jit(solution)/shard_map/ppermute | solution.py:16
  22.9 123.8 %copy-start.5 = (f32[1,128,512]{2,1,0:T(8,128)}, f32[1,128,512]{2,1,0:T(8,128)S(1)}, u32[]{:S(2)}) copy-start(f32[1,128,512]{2,1,0:T(8,128)S(1)} %collective-permute-done) | copy-start | bytes 786436
  22.9 10.2 %collective-permute-start.1 = (f32[1,128,512]{2,1,0:T(8,128)S(1)}, f32[1,128,512]{2,1,0:T(8,128)S(1)}, u32[]{:S(2)}, u32[]{:S(2)}) collective-permute-start(f32[1,128,512]{2,1,0:T(8,128)S(1)} %collective-permute-done), channel_id=1, source_target_pairs={{0,1},{1,2},{2,3},{3,4},{4,5},{5,6},{6,7},{7,0},{8,9},{9,10},{10,1... | collective-permute-start | bytes 786440 | tf_op jit(solution)/shard_map/ppermute | solution.py:16
  33.1 67.3 %collective-permute-start.2 = (f32[1,128,512]{2,1,0:T(8,128)S(1)}, f32[1,128,512]{2,1,0:T(8,128)S(1)}, u32[]{:S(2)}, u32[]{:S(2)}) collective-permute-start(f32[1,128,512]{2,1,0:T(8,128)S(1)} %collective-permute-done.1), channel_id=1, source_target_pairs={{0,1},{1,2},{2,3},{3,4},{4,5},{5,6},{6,7},{7,0},{8,9},{9,10},{10,1... | collective-permute-start | bytes 786440 | tf_op jit(solution)/shard_map/ppermute | solution.py:16
  35.2 126.5 %all-to-all-start = ((f32[8,128,128]{1,2,0:T(8,128)}), f32[8,128,128]{1,2,0:T(8,128)}, u32[]{:S(2)}, u32[]{:S(2)}) async-start(f32[8,128,128]{1,2,0:T(8,128)} %copy.9), calls=%async_computation | async-start | bytes 1048576 | tf_op jit(solution)/shard_map/all_to_all | solution.py:31
  41.2 114.2 %all-gather.3.cloned.1.call-start = ((), (), s32[]{:S(2)}) async-start(), calls=%async_computation.4 | async-start | bytes 1310720 | tf_op jit(solution)/shard_map/all_gather | solution.py:44
  100.3 59.2 %reduce-scatter.2.cloned.1.call-start = ((), (), s32[]{:S(2)}) async-start(), calls=%async_computation.3 | async-start | bytes 1310720 | tf_op jit(solution)/shard_map/reduce_scatter | solution.py:49
  100.3 12.2 %copy-start.1 = (f32[1024,1024]{1,0:T(8,128)S(1)}, f32[1024,1024]{1,0:T(8,128)}, u32[]{:S(2)}) copy-start(f32[1024,1024]{1,0:T(8,128)} %param.7) | copy-start | bytes 12582916
  100.4 10.7 %collective-permute-start.3 = (f32[1,128,512]{2,1,0:T(8,128)S(1)}, f32[1,128,512]{2,1,0:T(8,128)S(1)}, u32[]{:S(2)}, u32[]{:S(2)}) collective-permute-start(f32[1,128,512]{2,1,0:T(8,128)S(1)} %collective-permute-done.2), channel_id=1, source_target_pairs={{0,1},{1,2},{2,3},{3,4},{4,5},{5,6},{6,7},{7,0},{8,9},{9,10},{10,1... | collective-permute-start | bytes 786440 | tf_op jit(solution)/shard_map/ppermute | solution.py:16
  111.0 9.7 %copy-start.6 = (f32[1,128,512]{2,1,0:T(8,128)}, f32[1,128,512]{2,1,0:T(8,128)S(1)}, u32[]{:S(2)}) copy-start(f32[1,128,512]{2,1,0:T(8,128)S(1)} %collective-permute-done.3) | copy-start | bytes 786436
  111.0 9.7 %collective-permute-start.4 = (f32[1,128,512]{2,1,0:T(8,128)S(1)}, f32[1,128,512]{2,1,0:T(8,128)}, u32[]{:S(2)}, u32[]{:S(2)}) collective-permute-start(f32[1,128,512]{2,1,0:T(8,128)S(1)} %collective-permute-done.3), channel_id=1, source_target_pairs={{0,1},{1,2},{2,3},{3,4},{4,5},{5,6},{6,7},{7,0},{8,9},{9,10},{10,1... | collective-permute-start | bytes 786440 | tf_op jit(solution)/shard_map/ppermute | solution.py:16
  120.7 9.4 %collective-permute-start.5 = (f32[1,128,512]{2,1,0:T(8,128)}, f32[1,128,512]{2,1,0:T(8,128)}, u32[]{:S(2)}, u32[]{:S(2)}) collective-permute-start(f32[1,128,512]{2,1,0:T(8,128)} %collective-permute-done.4), channel_id=1, source_target_pairs={{0,1},{1,2},{2,3},{3,4},{4,5},{5,6},{6,7},{7,0},{8,9},{9,10},{10,1... | collective-permute-start | bytes 786440 | tf_op jit(solution)/shard_map/ppermute | solution.py:16
  123.4 6.8 %copy-start.3 = (f32[4,128,128]{1,2,0:T(8,128)}, f32[4,128,128]{1,2,0:T(8,128)S(1)}, u32[]{:S(2)}) copy-start(f32[4,128,128]{1,2,0:T(8,128)S(1)} %bitcast_multiply_fusion) | copy-start | bytes 786436
  123.4 21.2 %copy-start.7 = (f32[1,128,512]{2,1,0:T(8,128)S(1)}, f32[1,128,512]{2,1,0:T(8,128)}, u32[]{:S(2)}) copy-start(f32[1,128,512]{2,1,0:T(8,128)} %copy-done.6) | copy-start | bytes 786436
  130.2 9.4 %collective-permute-start.6 = (f32[1,128,512]{2,1,0:T(8,128)}, f32[1,128,512]{2,1,0:T(8,128)}, u32[]{:S(2)}, u32[]{:S(2)}) collective-permute-start(f32[1,128,512]{2,1,0:T(8,128)} %collective-permute-done.5), channel_id=1, source_target_pairs={{0,1},{1,2},{2,3},{3,4},{4,5},{5,6},{6,7},{7,0},{8,9},{9,10},{10,1... | collective-permute-start | bytes 786440 | tf_op jit(solution)/shard_map/ppermute | solution.py:16
  148.2 13.1 %copy-start.8 = (f32[1,128,128]{2,1,0:T(8,128)S(1)}, f32[1,128,128]{2,1,0:T(8,128)}, u32[]{:S(2)}) copy-start(f32[1,128,128]{2,1,0:T(8,128)} %param.10) | copy-start | bytes 196612
  161.3 3.8 %copy-start.4 = (f32[1024,128]{1,0:T(8,128)S(1)}, f32[1024,128]{1,0:T(8,128)}, u32[]{:S(2)}) copy-start(f32[1024,128]{1,0:T(8,128)} %param.8) | copy-start | bytes 1572868
  161.7 3.4 %copy-start.2 = (f32[1024,512]{1,0:T(8,128)S(1)}, f32[1024,512]{1,0:T(8,128)}, u32[]{:S(2)}) copy-start(f32[1024,512]{1,0:T(8,128)} %fusion.17) | copy-start | bytes 6291460
Sparse Core Ops, SparseCore 0:
  25.3 74.9 all-reduce.1
  101.8 16.0 all-gather.2
  133.3 26.1 reduce-scatter.1
